TPU v7x, 32 devices: a whole 2x2x4 slice. The times are simulated.
32 devices in a mesh: ep: 4 (over y, core), etp: 8 (over z, x).
Axes of the slice: x: 2, y: 2, z: 4, core: 2. Of those that a mesh axis runs over, the one named last changes fastest.
Arguments:
- tokens: bfloat16 [4096, 7168], P(('ep', 'etp')), may hold values from -6 to 6
- expert_ids: int32 [4096, 8], P(('ep', 'etp')), may hold values from 0 to 383, all different within a row; in each aligned block of 128 rows (0 to 127, 128 to 255, ...) at most 3 rows name the same one
- gate_q: int32 [4096, 8], P(('ep', 'etp')), may hold values from 1 to 1024
- w_gate: bfloat16 [4, 7168, 2048], P('ep', None, 'etp'), may hold values from -0.0625 to 0.0625
- w_up: bfloat16 [4, 7168, 2048], P('ep', None, 'etp'), may hold values from -0.0625 to 0.0625
- w_down: bfloat16 [4, 2048, 7168], P('ep', 'etp'), may hold values from -0.125 to 0.125
Outputs:
- mixed: bfloat16 [4096, 7168], P(('ep', 'etp'))
Inputs may be any that keep to these rules, and one draw needn't show every extreme that they name: `expert_ids`: each row names 8 different experts; among the 128 rows of one device no expert is named by more than 3 rows.
All inputs are finite; a program needn't handle non-finite values.
Results may differ from a plain program's by a relative error of at most 0.014.
Values may be sent and summed in bfloat16 or wider, within the bound.
A program may use at most 64 MiB of HBM per device.

v0:
```python
import jax
import jax.numpy as jnp
from jax import lax
from jax.sharding import PartitionSpec as P

CAP = 3


def body(tokens, expert_ids, gate_q, w_gate, w_up, w_down):
    groups = lax.axis_size("ep")
    members = lax.axis_size("etp")
    capacity = CAP
    width = tokens.shape[1]
    count_rows = tokens.shape[0]
    flat_ids = expert_ids.reshape(-1)
    owner_hot = (flat_ids[:, None] == jnp.arange(groups, dtype=jnp.int32)[None, :]).astype(
        jnp.int32
    )
    earlier = jnp.cumsum(owner_hot, axis=0) - owner_hot
    position = jnp.sum(earlier * owner_hot, axis=1)
    column = jnp.where(flat_ids < groups, flat_ids * capacity + position, -1)
    select = (column[:, None] == jnp.arange(groups * capacity, dtype=jnp.int32)[None, :]).astype(
        jnp.float32
    )
    select = select.reshape(count_rows, -1, groups * capacity)
    placing = jnp.sum(select, axis=1)
    gate_scale = gate_q.astype(jnp.float32) / 1024.0
    scaling = jnp.sum(select * gate_scale[:, :, None], axis=1)
    bucket = jnp.einsum(
        "tc,td->cd", placing.astype(jnp.bfloat16), tokens, preferred_element_type=jnp.float32
    )
    bucket = bucket.astype(jnp.bfloat16).reshape(groups, capacity, width)
    gathered = lax.all_gather(bucket, "etp", axis=1, tiled=True)
    arrived = lax.all_to_all(gathered, "ep", split_axis=0, concat_axis=0, tiled=True)
    gate = jnp.dot(arrived, w_gate[0], preferred_element_type=jnp.float32)
    upper = jnp.dot(arrived, w_up[0], preferred_element_type=jnp.float32)
    hidden = (jax.nn.silu(gate) * upper).astype(jnp.bfloat16)
    inner = hidden.shape[2]
    ordered = (
        hidden.reshape(groups, members, capacity, inner).transpose(1, 0, 2, 3).reshape(-1, inner)
    )
    term = jnp.dot(ordered, w_down[0], preferred_element_type=jnp.float32)
    rounded = lax.optimization_barrier(term.astype(jnp.bfloat16))
    summed = lax.psum_scatter(
        rounded.astype(jnp.float32).astype(jnp.bfloat16), "etp", scatter_dimension=0, tiled=True
    )
    local_out = summed.reshape(groups, capacity, width)
    results = lax.all_to_all(local_out, "ep", split_axis=0, concat_axis=0, tiled=True)
    flat_out = results.reshape(groups * capacity, width).astype(jnp.float32)
    mixed = jnp.dot(scaling, flat_out, precision=lax.Precision.HIGHEST)
    return mixed.astype(jnp.bfloat16)


def solution(mesh):
    in_specs = (
        P(("ep", "etp"), None),
        P(("ep", "etp"), None),
        P(("ep", "etp"), None),
        P("ep", None, "etp"),
        P("ep", None, "etp"),
        P("ep", "etp", None),
    )
    out_specs = P(("ep", "etp"), None)
    return jax.shard_map(body, mesh=mesh, in_specs=in_specs, out_specs=out_specs, check_vma=False)
```

profile of v0, /device:TPU:0, one launch (start us, length us, event | category | flops | bytes accessed | tf_op | source)
XLA Modules:
  0.0 157.0 jit_solution(10917868213449177721)
XLA Ops:
  6.5 0.9 copy.40
  7.5 0.1 eq.43
  7.6 0.1 eq.39
  7.7 1.1 reduce-window.6
  8.8 0.2 slice_reduce_fusion
  9.0 0.2 reduce-window.9
  9.2 0.1 add_bitcast_fusion
  9.3 0.1 reduce_sum.30
  9.4 0.7 add_select_fusion
  10.2 0.7 convert_multiply_fusion
  10.9 0.3 convolution_convert_fusion.2
  11.2 0.1 reshape.56
  11.4 0.8 copy.43
  12.2 45.0 %all-gather.2.cloned.1.call-done = bf16[4,24,7168]{2,0,1:T(4,128)(2,1)} async-done(((bf16[4,3,7168]{2,0,1:T(4,128)(2,1)}), bf16[4,24,7168]{2,0,1:T(4,128)(2,1)}) %all-gather.2.cloned.1.call-update) | async-done | bytes 1376272 | tf_op jit(solution)/shard_map/all_gather | solution.py:33
  57.2 1.9 %copy.44 = bf16[4,24,7168]{2,1,0:T(8,128)(2,1)S(1)} copy(bf16[4,24,7168]{2,0,1:T(4,128)(2,1)} %all-gather.2.cloned.1.call-done) | data formatting | bytes 2752512 | tf_op jit(solution)/shard_map/all_gather | solution.py:33
  59.1 20.5 %all_to_all.10 = bf16[4,24,7168]{2,1,0:T(8,128)(2,1)S(1)} all-to-all(bf16[4,24,7168]{2,1,0:T(8,128)(2,1)S(1)} %copy.44), channel_id=1, replica_groups=mesh['ep'=4,'etp'=8] {'ep'}, dimensions={0} | all-to-all | bytes 2752512 | tf_op jit(solution)/shard_map/all_to_all | solution.py:34
  79.6 0.7 fusion.4
  80.3 1.3 copy-done.2
  81.6 0.7 fusion.9
  82.5 2.8 %convolution_convert_fusion.1 = bf16[96,7168]{1,0:T(8,128)(2,1)S(1)} fusion(bf16[96,256]{1,0:T(8,128)(2,1)S(1)} %reshape.58, bf16[1,256,7168]{2,1,0:T(8,128)(2,1)} %param.11), kind=kOutput, calls=%fused_computation.1 | convolution fusion | flops 353009664 | bytes 5095424 | tf_op jit(solution)/shard_map/dot_general | solution.py:42
  85.3 43.2 %fusion = bf16[16,7168]{1,0:T(8,128)(2,1)S(1)} fusion(bf16[96,7168]{1,0:T(8,128)(2,1)S(1)} %convolution_convert_fusion.1), kind=kCustom, calls=%all-reduce-scatter | all-reduce-scatter fusion | flops 917505 | bytes 1606144
  128.5 1.5 collective-permute-start
  130.1 0.1 slice.9
  130.1 4.1 %collective-permute-start.1 = (bf16[12,7168]{1,0:T(8,128)(2,1)S(1)}, bf16[12,7168]{1,0:T(8,128)(2,1)S(1)}, u32[]{:S(2)}, u32[]{:S(2)}) collective-permute-start(bf16[12,7168]{1,0:T(8,128)(2,1)S(1)} %slice.9), channel_id=1, source_target_pairs={{0,2},{1,3},{2,4},{3,5},{4,6},{5,7},{8,10},{9,11},{10,12},{11,13},... | collective-permute-start | bytes 516104
  134.2 0.6 dynamic-slice.4
  135.4 2.3 %collective-permute-done.1 = bf16[12,7168]{1,0:T(8,128)(2,1)S(1)} collective-permute-done((bf16[12,7168]{1,0:T(8,128)(2,1)S(1)}, bf16[12,7168]{1,0:T(8,128)(2,1)S(1)}, u32[]{:S(2)}, u32[]{:S(2)}) %collective-permute-start.1) | collective-permute-done | bytes 172064
  137.7 1.2 concatenate
  138.9 0.1 constant_dynamic-slice_fusion
  139.0 0.1 reshape.59
  139.1 8.0 %all_to_all.11 = bf16[4,3,7168]{2,1,0:T(4,128)(2,1)S(1)} all-to-all(bf16[4,3,7168]{2,1,0:T(4,128)(2,1)S(1)} %reshape.59), channel_id=1, replica_groups=mesh['ep'=4,'etp'=8] {'ep'}, dimensions={0} | all-to-all | bytes 344064 | tf_op jit(solution)/shard_map/all_to_all | solution.py:48
  147.1 0.2 reshape.60
  147.3 2.9 %convolution_convert_fusion = bf16[128,7168]{1,0:T(8,128)(2,1)} fusion(f32[128,12]{0,1:T(8,128)S(1)} %get-tuple-element.6, bf16[12,7168]{1,0:T(8,128)(2,1)S(1)} %reshape.60), kind=kOutput, calls=%fused_computation | convolution fusion | flops 133038080 | bytes 2013184 | tf_op jit(solution)/shard_map/dot_general | solution.py:50
  (17 shorter events, 0.2 us)
Async XLA Ops:
  6.5 4.4 %copy-start = (bf16[128,7168]{1,0:T(8,128)(2,1)S(1)}, bf16[128,7168]{1,0:T(8,128)(2,1)}, u32[]{:S(2)}) copy-start(bf16[128,7168]{1,0:T(8,128)(2,1)} %param.6) | copy-start | bytes 5505028
  6.5 50.7 %all-gather.2.cloned.1.call-start = ((), (), s32[]{:S(2)}) async-start(), calls=%async_computation.2 | async-start | bytes 1548288 | tf_op jit(solution)/shard_map/all_gather | solution.py:33
  57.2 22.4 %copy-start.1 = (bf16[1,7168,256]{2,1,0:T(8,128)(2,1)S(1)}, bf16[1,7168,256]{2,1,0:T(8,128)(2,1)}, u32[]{:S(2)}) copy-start(bf16[1,7168,256]{2,1,0:T(8,128)(2,1)} %param.9) | copy-start | bytes 11010052
  79.6 2.0 %copy-start.2 = (bf16[1,7168,256]{2,1,0:T(8,128)(2,1)S(1)}, bf16[1,7168,256]{2,1,0:T(8,128)(2,1)}, u32[]{:S(2)}) copy-start(bf16[1,7168,256]{2,1,0:T(8,128)(2,1)} %param.10) | copy-start | bytes 11010052
  85.2 48.9 %copy-start.3 = (u32[32]{0:T(128)S(1)}, u32[32]{0:T(128)}, u32[]{:S(2)}) copy-start(u32[32]{0:T(128)} %constant.26) | copy-start | bytes 388
  128.5 9.2 %collective-permute-start = (bf16[16,7168]{1,0:T(8,128)(2,1)S(1)}, bf16[16,7168]{1,0:T(8,128)(2,1)S(1)}, u32[]{:S(2)}, u32[]{:S(2)}) collective-permute-start(bf16[16,7168]{1,0:T(8,128)(2,1)S(1)} %fusion), channel_id=1, source_target_pairs={{0,1},{1,2},{2,3},{3,4},{4,5},{5,6},{6,7},{8,9},{9,10},{10,11},{11... | collective-permute-start | bytes 688136
  130.1 7.6 %collective-permute-start.1 = (bf16[12,7168]{1,0:T(8,128)(2,1)S(1)}, bf16[12,7168]{1,0:T(8,128)(2,1)S(1)}, u32[]{:S(2)}, u32[]{:S(2)}) collective-permute-start(bf16[12,7168]{1,0:T(8,128)(2,1)S(1)} %slice.9), channel_id=1, source_target_pairs={{0,2},{1,3},{2,4},{3,5},{4,6},{5,7},{8,10},{9,11},{10,12},{11,13},... | collective-permute-start | bytes 516104
Sparse Core Ops, SparseCore 0:
  12.3 44.8 all-gather.1
where the time goes:
time: 157 us
  blocking collectives  71.8 us (46%)
  waiting for transfers between devices  47.3 us (30%)
  between operations  14.2 us (9%)
  local copies, waits for them, and re-layouts  7.82 us (5%)
  matrix products  7.42 us (5%)
  starting transfers between devices  5.6 us (4%)
  other arithmetic  2.87 us (2%)
    all_gather x1, waiting for transfers between devices, body(): gathered = lax.all_gather(bucket, 'etp', axis=1, tiled=True)  45 us
    unnamed x1, blocking collectives  43.2 us
    all_to_all x1, blocking collectives, body(): lax.all_to_all(gathered, 'ep', split_axis=0, concat_axis=0, tiled=True)  20.5 us
    all_to_all x1, blocking collectives, body(): lax.all_to_all(local_out, 'ep', split_axis=0, concat_axis=0, tiled=True)  8.03 us
    unnamed x2, starting transfers between devices  5.6 us
    unnamed x13, local copies, waits for them, and re-layouts  4.14 us
  transfers between devices with their start and end apart: 3, of which 2 were waited for; matrix products, arithmetic and copies ran while one was open for 0% of the time, Pallas kernels for 0%

commit v1 on v0

--- a/solution.py
+++ b/solution.py
@@ -4,6 +4,17 @@
 from jax.sharding import PartitionSpec as P
 
 CAP = 3
+
+
+def divide_core(message, array_dim, s0):
+    newest, carry = (message.shape[:array_dim], message.shape[array_dim + 1 :])
+    return jnp.moveaxis(message.reshape(*newest, s0, -1, *carry), array_dim, 0)
+
+
+def change_records_for(xx, along_dim):
+    y = list(xx.shape[1:])
+    y[along_dim] *= xx.shape[0]
+    return jnp.moveaxis(xx, 0, along_dim).reshape(y)
 
 
 def body(tokens, expert_ids, gate_q, w_gate, w_up, w_down):
@@ -45,7 +56,14 @@
         rounded.astype(jnp.float32).astype(jnp.bfloat16), "etp", scatter_dimension=0, tiled=True
     )
     local_out = summed.reshape(groups, capacity, width)
-    results = lax.all_to_all(local_out, "ep", split_axis=0, concat_axis=0, tiled=True)
+    w1, piece_now = (lax.axis_size("ep"), lax.axis_index("ep"))
+    found_now = divide_core(local_out, 0, w1)
+    slots = [found_now[piece_now]]
+    for ix in tuple(range(1, w1)):
+        part_now = found_now[piece_now ^ ix]
+        slots.append(lax.ppermute(part_now, "ep", [(hop_no, hop_no ^ ix) for hop_no in range(w1)]))
+    found_now = jnp.stack(slots, 0)[piece_now ^ jnp.arange(w1)]
+    results = change_records_for(found_now, 0)
     flat_out = results.reshape(groups * capacity, width).astype(jnp.float32)
     mixed = jnp.dot(scaling, flat_out, precision=lax.Precision.HIGHEST)
     return mixed.astype(jnp.bfloat16)

time: 157 us -> 155 us (0.987)
  blocking collectives: 71.8 us -> 63.7 us
  waiting for transfers between devices: 47.3 us -> 50.2 us
  starting transfers between devices: 5.6 us -> 7.51 us
    all_to_all x1 -> x0, blocking collectives: 8.03 us -> none  [body(): lax.all_to_all(local_out, 'ep', split_axis=0, concat_axis=0, tiled=True)]
    ppermute x0 -> x3, waiting for transfers between devices: none -> 2.97 us  [body(): lax.ppermute(part_now, 'ep', [(hop_no, hop_no ^ ix) for hop_no in range(w...]
    ppermute x0 -> x3, starting transfers between devices: none -> 1.91 us  [body(): lax.ppermute(part_now, 'ep', [(hop_no, hop_no ^ ix) for hop_no in range(w...]
  transfers between devices with their start and end apart: 3 -> 6, of which waited for: 2 -> 4; matrix products, arithmetic and copies ran while one was open for 0% -> 0% of each run, Pallas kernels for 0% -> 0%
where the time goes in v1:
time: 155 us
  blocking collectives  63.7 us (41%)
  waiting for transfers between devices  50.2 us (32%)
  between operations  14.3 us (9%)
  local copies, waits for them, and re-layouts  8.66 us (6%)
  starting transfers between devices  7.51 us (5%)
  matrix products  7.42 us (5%)
  other arithmetic  3.09 us (2%)
    all_gather x1, waiting for transfers between devices, body(): gathered = lax.all_gather(bucket, 'etp', axis=1, tiled=True)  45 us
    unnamed x1, blocking collectives  43.2 us
    all_to_all x1, blocking collectives, body(): lax.all_to_all(gathered, 'ep', split_axis=0, concat_axis=0, tiled=True)  20.5 us
    unnamed x2, starting transfers between devices  5.6 us
    unnamed x13, local copies, waits for them, and re-layouts  4.14 us
  transfers between devices with their start and end apart: 6, of which 4 were waited for; matrix products, arithmetic and copies ran while one was open for 0% of the time, Pallas kernels for 0%

profile of v1, /device:TPU:0, one launch (start us, length us, event | category | flops | bytes accessed | tf_op | source)
XLA Modules:
  0.0 154.9 jit_solution(2643849074247078757)
XLA Ops:
  6.5 0.9 copy.40
  7.5 0.1 eq.43
  7.7 1.1 reduce-window.6
  8.8 0.2 slice_reduce_fusion
  9.0 0.2 reduce-window.9
  9.4 0.7 add_select_fusion
  10.2 0.7 convert_multiply_fusion
  10.9 0.3 convolution_convert_fusion.2
  11.2 0.1 reshape.66
  11.4 0.8 copy.43
  12.2 45.0 %all-gather.2.cloned.1.call-done = bf16[4,24,7168]{2,0,1:T(4,128)(2,1)} async-done(((bf16[4,3,7168]{2,0,1:T(4,128)(2,1)}), bf16[4,24,7168]{2,0,1:T(4,128)(2,1)}) %all-gather.2.cloned.1.call-update) | async-done | bytes 1376272 | tf_op jit(solution)/shard_map/all_gather | solution.py:44
  57.2 1.9 %copy.44 = bf16[4,24,7168]{2,1,0:T(8,128)(2,1)S(1)} copy(bf16[4,24,7168]{2,0,1:T(4,128)(2,1)} %all-gather.2.cloned.1.call-done) | data formatting | bytes 2752512 | tf_op jit(solution)/shard_map/all_gather | solution.py:44
  59.1 20.5 %all_to_all.5 = bf16[4,24,7168]{2,1,0:T(8,128)(2,1)S(1)} all-to-all(bf16[4,24,7168]{2,1,0:T(8,128)(2,1)S(1)} %copy.44), channel_id=1, replica_groups=mesh['ep'=4,'etp'=8] {'ep'}, dimensions={0} | all-to-all | bytes 2752512 | tf_op jit(solution)/shard_map/all_to_all | solution.py:45
  79.6 0.7 fusion.4
  80.3 1.3 copy-done.2
  81.6 0.7 fusion.9
  82.5 2.8 %convolution_convert_fusion.1 = bf16[96,7168]{1,0:T(8,128)(2,1)S(1)} fusion(bf16[96,256]{1,0:T(8,128)(2,1)S(1)} %reshape.68, bf16[1,256,7168]{2,1,0:T(8,128)(2,1)} %param.11), kind=kOutput, calls=%fused_computation.2 | convolution fusion | flops 353009664 | bytes 5095424 | tf_op jit(solution)/shard_map/dot_general | solution.py:53
  85.3 43.2 %fusion = bf16[16,7168]{1,0:T(8,128)(2,1)S(1)} fusion(bf16[96,7168]{1,0:T(8,128)(2,1)S(1)} %convolution_convert_fusion.1), kind=kCustom, calls=%all-reduce-scatter | all-reduce-scatter fusion | flops 917505 | bytes 1606144
  128.5 1.5 collective-permute-start.3
  130.1 4.1 %collective-permute-start.4 = (bf16[12,7168]{1,0:T(8,128)(2,1)S(1)}, bf16[12,7168]{1,0:T(8,128)(2,1)S(1)}, u32[]{:S(2)}, u32[]{:S(2)}) collective-permute-start(bf16[12,7168]{1,0:T(8,128)(2,1)S(1)} %slice.11), channel_id=1, source_target_pairs={{0,2},{1,3},{2,4},{3,5},{4,6},{5,7},{8,10},{9,11},{10,12},{11,13},... | collective-permute-start | bytes 516104
  134.2 0.6 dynamic-slice.4
  135.5 2.2 %collective-permute-done.4 = bf16[12,7168]{1,0:T(8,128)(2,1)S(1)} collective-permute-done((bf16[12,7168]{1,0:T(8,128)(2,1)S(1)}, bf16[12,7168]{1,0:T(8,128)(2,1)S(1)}, u32[]{:S(2)}, u32[]{:S(2)}) %collective-permute-start.4) | collective-permute-done | bytes 172064
  137.7 1.2 concatenate
  139.0 0.1 reshape_reshape.6
  139.1 0.1 constant_dynamic-slice_fusion.1
  139.4 1.8 %collective-permute-start = (bf16[1,3,7168]{2,1,0:T(4,128)(2,1)S(1)}, bf16[1,3,7168]{2,1,0:T(4,128)(2,1)S(1)}, u32[]{:S(2)}, u32[]{:S(2)}) collective-permute-start(bf16[1,3,7168]{2,1,0:T(4,128)(2,1)S(1)} %get-tuple-element.10), channel_id=1, source_target_pairs={{0,8},{8,0},{16,24},{24,16},{1,9},{9,1},{17,25},{25,17},{2,10},{10... | collective-permute-start | bytes 129032 | tf_op jit(solution)/shard_map/ppermute | solution.py:64
  141.1 1.7 %collective-permute-done.2 = bf16[1,3,7168]{2,1,0:T(4,128)(2,1)S(1)} collective-permute-done((bf16[1,3,7168]{2,1,0:T(4,128)(2,1)S(1)}, bf16[1,3,7168]{2,1,0:T(4,128)(2,1)S(1)}, u32[]{:S(2)}, u32[]{:S(2)}) %collective-permute-start.2) | collective-permute-done | bytes 43040 | tf_op jit(solution)/shard_map/ppermute | solution.py:64
  142.9 1.2 collective-permute-done.1
  144.1 0.2 maximum_bitcast_fusion
  144.3 0.7 gather_fusion
  145.1 0.2 reshape_reshape.7
  145.2 2.9 %convolution_convert_fusion = bf16[128,7168]{1,0:T(8,128)(2,1)} fusion(f32[128,12]{0,1:T(8,128)S(1)} %get-tuple-element.6, bf16[12,7168]{1,0:T(8,128)(2,1)S(1)} %reshape_reshape.7), kind=kOutput, calls=%fused_computation.1 | convolution fusion | flops 133038080 | bytes 2013184 | tf_op jit(solution)/shard_map/dot_general | solution.py:68
  (27 shorter events, 0.8 us)
Async XLA Ops:
  6.5 4.4 %copy-start = (bf16[128,7168]{1,0:T(8,128)(2,1)S(1)}, bf16[128,7168]{1,0:T(8,128)(2,1)}, u32[]{:S(2)}) copy-start(bf16[128,7168]{1,0:T(8,128)(2,1)} %param.6) | copy-start | bytes 5505028
  6.5 50.7 %all-gather.2.cloned.1.call-start = ((), (), s32[]{:S(2)}) async-start(), calls=%async_computation.1 | async-start | bytes 1548288 | tf_op jit(solution)/shard_map/all_gather | solution.py:44
  57.2 22.4 %copy-start.1 = (bf16[1,7168,256]{2,1,0:T(8,128)(2,1)S(1)}, bf16[1,7168,256]{2,1,0:T(8,128)(2,1)}, u32[]{:S(2)}) copy-start(bf16[1,7168,256]{2,1,0:T(8,128)(2,1)} %param.9) | copy-start | bytes 11010052
  79.6 2.0 %copy-start.2 = (bf16[1,7168,256]{2,1,0:T(8,128)(2,1)S(1)}, bf16[1,7168,256]{2,1,0:T(8,128)(2,1)}, u32[]{:S(2)}) copy-start(bf16[1,7168,256]{2,1,0:T(8,128)(2,1)} %param.10) | copy-start | bytes 11010052
  85.2 49.0 %copy-start.3 = (u32[32]{0:T(128)S(1)}, u32[32]{0:T(128)}, u32[]{:S(2)}) copy-start(u32[32]{0:T(128)} %constant.39) | copy-start | bytes 388
  128.5 9.2 %collective-permute-start.3 = (bf16[16,7168]{1,0:T(8,128)(2,1)S(1)}, bf16[16,7168]{1,0:T(8,128)(2,1)S(1)}, u32[]{:S(2)}, u32[]{:S(2)}) collective-permute-start(bf16[16,7168]{1,0:T(8,128)(2,1)S(1)} %fusion), channel_id=1, source_target_pairs={{0,1},{1,2},{2,3},{3,4},{4,5},{5,6},{6,7},{8,9},{9,10},{10,11},{11... | collective-permute-start | bytes 688136
  130.1 7.6 %collective-permute-start.4 = (bf16[12,7168]{1,0:T(8,128)(2,1)S(1)}, bf16[12,7168]{1,0:T(8,128)(2,1)S(1)}, u32[]{:S(2)}, u32[]{:S(2)}) collective-permute-start(bf16[12,7168]{1,0:T(8,128)(2,1)S(1)} %slice.11), channel_id=1, source_target_pairs={{0,2},{1,3},{2,4},{3,5},{4,6},{5,7},{8,10},{9,11},{10,12},{11,13},... | collective-permute-start | bytes 516104
  139.2 3.7 %collective-permute-start.2 = (bf16[1,3,7168]{2,1,0:T(4,128)(2,1)S(1)}, bf16[1,3,7168]{2,1,0:T(4,128)(2,1)S(1)}, u32[]{:S(2)}, u32[]{:S(2)}) collective-permute-start(bf16[1,3,7168]{2,1,0:T(4,128)(2,1)S(1)} %get-tuple-element.8), channel_id=1, source_target_pairs={{0,24},{8,16},{16,8},{24,0},{1,25},{9,17},{17,9},{25,1},{2,26},{10... | collective-permute-start | bytes 129032 | tf_op jit(solution)/shard_map/ppermute | solution.py:64
  139.3 4.8 %collective-permute-start.1 = (bf16[1,3,7168]{2,1,0:T(4,128)(2,1)S(1)}, bf16[1,3,7168]{2,1,0:T(4,128)(2,1)S(1)}, u32[]{:S(2)}, u32[]{:S(2)}) collective-permute-start(bf16[1,3,7168]{2,1,0:T(4,128)(2,1)S(1)} %get-tuple-element.9), channel_id=1, source_target_pairs={{0,16},{8,24},{16,0},{24,8},{1,17},{9,25},{17,1},{25,9},{2,18},{10... | collective-permute-start | bytes 129032 | tf_op jit(solution)/shard_map/ppermute | solution.py:64
  139.4 4.7 %collective-permute-start = (bf16[1,3,7168]{2,1,0:T(4,128)(2,1)S(1)}, bf16[1,3,7168]{2,1,0:T(4,128)(2,1)S(1)}, u32[]{:S(2)}, u32[]{:S(2)}) collective-permute-start(bf16[1,3,7168]{2,1,0:T(4,128)(2,1)S(1)} %get-tuple-element.10), channel_id=1, source_target_pairs={{0,8},{8,0},{16,24},{24,16},{1,9},{9,1},{17,25},{25,17},{2,10},{10... | collective-permute-start | bytes 129032 | tf_op jit(solution)/shard_map/ppermute | solution.py:64
Sparse Core Ops, SparseCore 0:
  12.3 44.8 all-gather.1
